TPU v7x, 32 devices: a whole 2x2x4 slice. The times are simulated.
32 devices in a mesh: gx: 4 (over x, core), gy: 4 (over z), gz: 2 (over y).
Axes of the slice: x: 2, y: 2, z: 4, core: 2. Of those that a mesh axis runs over, the one named last changes fastest.
Arguments:
- density: float32 [16, 128, 256], P('gx', 'gy', 'gz'), may hold values from 0.5 to 2
- velocity: float32 [3, 16, 128, 256], P(None, 'gx', 'gy', 'gz'), may hold values from -2.5 to 2.5
- pressure: float32 [16, 128, 256], P('gx', 'gy', 'gz'), may hold values from 0.5 to 2
Outputs:
- section_state: float32 [5, 16, 128, 256], P(None, 'gx', 'gy', 'gz')
All inputs are finite; a program needn't handle non-finite values.
Results may differ from a plain program's by a relative error of at most 0.0003.
Values sent between devices are 32-bit elements; how exact they have to be, the bound alone decides.
A program may use at most 64 MiB of HBM per device.

v0:
```python
import jax
import jax.numpy as jnp
from jax import lax
from jax.sharding import PartitionSpec as P

gamma_gas = 1.4
weno_eps = 1e-06
cfl_number = 0.4


def padded_2(cells, sides, width):
    for axis, dim in sides:
        count = lax.axis_size(axis)
        head = lax.slice_in_dim(cells, 0, width, axis=dim)
        tail = lax.slice_in_dim(cells, cells.shape[dim] - width, cells.shape[dim], axis=dim)
        cells = jnp.concatenate(
            [
                lax.ppermute(tail, axis, [(i, (i + 1) % count) for i in range(count)]),
                cells,
                lax.ppermute(head, axis, [((i + 1) % count, i) for i in range(count)]),
            ],
            axis=dim,
        )
    return cells


def conserved(density, velocity, pressure):
    momenta = density[None] * velocity
    kinetic = 0.5 * density * jnp.sum(velocity * velocity, axis=0)
    energy = pressure / (gamma_gas - 1.0) + kinetic
    return jnp.concatenate([density[None], momenta, energy[None]], axis=0)


def wave_speed(density, velocity, pressure):
    sound = jnp.sqrt(gamma_gas * pressure / density)
    return jnp.max(jnp.sum(jnp.abs(velocity), axis=0) + 3.0 * sound)


def combine(coeffs, arrays):
    total = None
    for coeff, array in zip(coeffs, arrays):
        if isinstance(coeff, float) and coeff == 0.0:
            continue
        term = coeff * array
        total = term if total is None else total + term
    return total


def weno_face(values):
    first, second, third, fourth, fifth = values
    cand_left = (2.0 * first - 7.0 * second + 11.0 * third) / 6.0
    cand_middle = (-second + 5.0 * third + 2.0 * fourth) / 6.0
    cand_right = (2.0 * third + 5.0 * fourth - fifth) / 6.0
    smooth_left = (
        13.0 / 12.0 * (first - 2.0 * second + third) ** 2
        + 0.25 * (first - 4.0 * second + 3.0 * third) ** 2
    )
    smooth_middle = (
        13.0 / 12.0 * (second - 2.0 * third + fourth) ** 2 + 0.25 * (second - fourth) ** 2
    )
    smooth_right = (
        13.0 / 12.0 * (third - 2.0 * fourth + fifth) ** 2
        + 0.25 * (3.0 * third - 4.0 * fourth + fifth) ** 2
    )
    weight_left = 0.1 / (weno_eps + smooth_left) ** 2
    weight_middle = 0.6 / (weno_eps + smooth_middle) ** 2
    weight_right = 0.3 / (weno_eps + smooth_right) ** 2
    return (weight_left * cand_left + weight_middle * cand_middle + weight_right * cand_right) / (
        weight_left + weight_middle + weight_right
    )


def direction_flux(padded, field_dim, normal_comp):
    cells = padded.shape[field_dim + 1] - 6
    faces = cells + 1
    density = padded[0]
    energy = padded[4]
    velocity = [padded[1 + member] / density for member in range(3)]
    speed_sq = velocity[0] * velocity[0] + velocity[1] * velocity[1] + velocity[2] * velocity[2]
    pressure = (gamma_gas - 1.0) * (energy - 0.5 * density * speed_sq)
    sound_sq = gamma_gas * pressure / density
    sound = jnp.sqrt(sound_sq)
    enthalpy = (energy + pressure) / density
    normal_vel = velocity[normal_comp]
    others = [member for member in range(3) if member != normal_comp]
    order = [0, 1 + normal_comp, 1 + others[0], 1 + others[1], 4]
    state_perm = [padded[member] for member in order]
    flux_perm = [
        density * normal_vel,
        padded[1 + normal_comp] * normal_vel + pressure,
        padded[1 + others[0]] * normal_vel,
        padded[1 + others[1]] * normal_vel,
        (energy + pressure) * normal_vel,
    ]
    signal = jnp.abs(normal_vel) + sound

    def window(array, offset):
        return lax.slice_in_dim(array, offset, offset + faces, axis=field_dim)

    root_left = jnp.sqrt(window(density, 2))
    root_right = jnp.sqrt(window(density, 3))
    share_left = root_left / (root_left + root_right)
    share_right = root_right / (root_left + root_right)
    roe_vel = [
        share_left * window(member, 2) + share_right * window(member, 3) for member in velocity
    ]
    roe_enth = share_left * window(enthalpy, 2) + share_right * window(enthalpy, 3)
    jump_sq = sum(((window(member, 3) - window(member, 2)) ** 2 for member in velocity))
    roe_sound_sq = (
        share_left * window(sound_sq, 2)
        + share_right * window(sound_sq, 3)
        + 0.5 * (gamma_gas - 1.0) * share_left * share_right * jump_sq
    )
    roe_sound = jnp.sqrt(roe_sound_sq)
    normal_roe = roe_vel[normal_comp]
    tang_first = roe_vel[others[0]]
    tang_second = roe_vel[others[1]]
    roe_qsq = normal_roe * normal_roe + tang_first * tang_first + tang_second * tang_second
    b_one = (gamma_gas - 1.0) / roe_sound_sq
    b_two = 0.5 * b_one * roe_qsq
    inv_sound = 1.0 / roe_sound
    left_rows = [
        [
            0.5 * (b_two + normal_roe * inv_sound),
            -0.5 * (b_one * normal_roe + inv_sound),
            -0.5 * b_one * tang_first,
            -0.5 * b_one * tang_second,
            0.5 * b_one,
        ],
        [1.0 - b_two, b_one * normal_roe, b_one * tang_first, b_one * tang_second, -b_one],
        [-tang_first, 0.0, 1.0, 0.0, 0.0],
        [-tang_second, 0.0, 0.0, 1.0, 0.0],
        [
            0.5 * (b_two - normal_roe * inv_sound),
            -0.5 * (b_one * normal_roe - inv_sound),
            -0.5 * b_one * tang_first,
            -0.5 * b_one * tang_second,
            0.5 * b_one,
        ],
    ]
    right_rows = [
        [1.0, 1.0, 0.0, 0.0, 1.0],
        [normal_roe - roe_sound, normal_roe, 0.0, 0.0, normal_roe + roe_sound],
        [tang_first, tang_first, 1.0, 0.0, tang_first],
        [tang_second, tang_second, 0.0, 1.0, tang_second],
        [
            roe_enth - normal_roe * roe_sound,
            0.5 * roe_qsq,
            tang_first,
            tang_second,
            roe_enth + normal_roe * roe_sound,
        ],
    ]
    alpha = window(signal, 0)
    for offset in range(1, 6):
        alpha = jnp.maximum(alpha, window(signal, offset))
    plus_vals = [[None] * 6 for member in range(5)]
    minus_vals = [[None] * 6 for member in range(5)]
    for offset in range(6):
        state_here = [window(member, offset) for member in state_perm]
        flux_here = [window(member, offset) for member in flux_perm]
        for charac in range(5):
            char_state = combine(left_rows[charac], state_here)
            char_flux = combine(left_rows[charac], flux_here)
            plus_vals[charac][offset] = 0.5 * (char_flux + alpha * char_state)
            minus_vals[charac][offset] = 0.5 * (char_flux - alpha * char_state)
    hats = []
    for charac in range(5):
        upwind = weno_face(plus_vals[charac][0:5])
        downwind = weno_face(
            [
                minus_vals[charac][5],
                minus_vals[charac][4],
                minus_vals[charac][3],
                minus_vals[charac][2],
                minus_vals[charac][1],
            ]
        )
        hats.append(upwind + downwind)
    face_flux = [None] * 5
    for member in range(5):
        face_flux[order[member]] = combine(right_rows[member], hats)
    result = [
        lax.slice_in_dim(member, 1, faces, axis=field_dim)
        - lax.slice_in_dim(member, 0, faces - 1, axis=field_dim)
        for member in face_flux
    ]
    return jnp.stack(result, axis=0)


def local(density, velocity, pressure):
    state = conserved(density, velocity, pressure)
    local_top = wave_speed(density, velocity, pressure)
    top = lax.pmax(local_top, ("gx", "gy", "gz"))
    along_first = padded_2(state, (("gx", 1),), 3)
    along_second = padded_2(state, (("gy", 2),), 3)
    along_third = padded_2(state, (("gz", 3),), 3)
    total = direction_flux(along_first, 0, 0)
    total = total + direction_flux(along_second, 1, 1)
    total = total + direction_flux(along_third, 2, 2)
    step = cfl_number / top
    return state - step * total


def solution(mesh):
    in_specs = (P("gx", "gy", "gz"), P(None, "gx", "gy", "gz"), P("gx", "gy", "gz"))
    out_specs = P(None, "gx", "gy", "gz")
    return jax.shard_map(local, mesh=mesh, in_specs=in_specs, out_specs=out_specs, check_vma=False)
```

profile of v0, /device:TPU:1, one launch (start us, length us, event | category | flops | bytes accessed | tf_op | source)
XLA Modules:
  0.0 78.7 jit_solution(17060478465141477660)
XLA Ops:
  0.0 0.0 copy-start
  0.0 0.0 copy-start.1
  0.0 1.0 %abs_reduce_fusion = (f32[4,32,128]{2,1,0:T(8,128)S(1)}, f32[4,32,128]{2,1,0:T(8,128)S(1)}, f32[3,4,32,128]{3,2,1,0:T(8,128)S(1)}) fusion(f32[3,4,32,128]{3,2,1,0:T(8,128)} %param.4, f32[4,32,128]{2,1,0:T(8,128)} %param.3), kind=kLoop, calls=%fused_computation.7 | loop fusion | flops 212992 | bytes 589824 | tf_op jit(solution)/shard_map/reduce_sum | solution.py:36
  1.0 0.0 copy-done
  1.0 0.0 copy-done.1
  1.0 0.6 add_reduce_fusion
  1.7 0.2 fusion.149
  1.9 2.1 %collective-permute-start.5 = (f32[5,4,32,3]{3,2,1,0:T(8,128)S(1)}, f32[5,4,32,3]{3,2,1,0:T(8,128)S(1)}, u32[]{:S(2)}, u32[]{:S(2)}) collective-permute-start(f32[5,4,32,3]{3,2,1,0:T(8,128)S(1)} %get-tuple-element.103), channel_id=1, source_target_pairs={{1,0},{0,1},{3,2},{2,3},{5,4},{4,5},{7,6},{6,7},{9,8},{8,9},{11,10... | collective-permute-start | bytes 23048 | tf_op jit(solution)/shard_map/ppermute | solution.py:20
  4.0 0.1 collective-permute-start.4
  4.1 3.5 %collective-permute-start.3 = (f32[5,4,3,128]{3,2,1,0:T(4,128)S(1)}, f32[5,4,3,128]{3,2,1,0:T(4,128)S(1)}, u32[]{:S(2)}, u32[]{:S(2)}) collective-permute-start(f32[5,4,3,128]{3,2,1,0:T(4,128)S(1)} %get-tuple-element.97), channel_id=1, source_target_pairs={{2,0},{4,2},{6,4},{0,6},{3,1},{5,3},{7,5},{1,7},{10,8},{12,10},{14... | collective-permute-start | bytes 92168 | tf_op jit(solution)/shard_map/ppermute | solution.py:20
  7.6 0.0 collective-permute-start.2
  7.7 1.6 %collective-permute-start.1 = (f32[5,3,32,128]{3,2,1,0:T(8,128)S(1)}, f32[5,3,32,128]{3,2,1,0:T(8,128)S(1)}, u32[]{:S(2)}, u32[]{:S(2)}) collective-permute-start(f32[5,3,32,128]{3,2,1,0:T(8,128)S(1)} %get-tuple-element.101), channel_id=1, source_target_pairs={{8,0},{16,8},{24,16},{0,24},{9,1},{17,9},{25,17},{1,25},{10,2},{18... | collective-permute-start | bytes 737288 | tf_op jit(solution)/shard_map/ppermute | solution.py:20
  9.2 43.8 %pmax.7 = f32[]{:T(128)} all-reduce(f32[]{:T(128)} %get-tuple-element.116), channel_id=1, replica_groups=mesh['gx'=4,'gy'=4,'gz'=2] {'gx','gy','gz'}, use_global_device_ids=true, to_apply=%region_3.0 | all-reduce | flops 1 | bytes 8 | tf_op jit(solution)/shard_map/pmax | solution.py:194
  53.8 0.0 collective-permute-done.5
  53.8 3.2 %collective-permute-start = (f32[5,3,32,128]{3,2,1,0:T(8,128)S(1)}, f32[5,3,32,128]{3,2,1,0:T(8,128)S(1)}, u32[]{:S(2)}, u32[]{:S(2)}) collective-permute-start(f32[5,3,32,128]{3,2,1,0:T(8,128)S(1)} %get-tuple-element.100), channel_id=1, source_target_pairs={{0,8},{8,16},{16,24},{24,0},{1,9},{9,17},{17,25},{25,1},{2,10},{10... | collective-permute-start | bytes 737288 | tf_op jit(solution)/shard_map/ppermute | solution.py:18
  57.0 0.0 collective-permute-done.4
  57.0 0.3 pad_maximum_fusion.1
  57.4 0.1 slice_bitcast_fusion.5
  57.4 0.1 fusion.120
  57.5 0.2 add_divide_fusion.1
  57.7 0.1 fusion.129
  57.8 9.1 %multiply_add_fusion.3 = (f32[4,32,129]{2,1,0:T(8,128)S(1)}, f32[4,32,129]{2,1,0:T(8,128)S(1)}, f32[4,32,129]{2,1,0:T(8,128)S(1)}, f32[4,32,129]{2,1,0:T(8,128)S...) fusion(f32[4,32,129]{2,1,0:T(8,128)S(1)} %get-tuple-element.119, ...), kind=kLoop, calls=%fused_computation.47 | loop fusion | flops 18889728 | bytes 5812224 | tf_op jit(solution)/shard_map/add | solution.py:45
  66.9 0.1 multiply_add_fusion.4
  67.1 0.1 fusion.98
  67.1 0.1 fusion.96
  67.2 0.1 fusion.94
  67.3 0.1 fusion.92
  67.4 0.0 collective-permute-done.3
  67.4 0.0 collective-permute-done.2
  67.4 0.1 pad_maximum_fusion.3
  67.5 0.1 fusion.122
  67.6 0.1 add_divide_fusion.3
  67.7 0.1 fusion.124
  67.7 4.6 %multiply_add_fusion.15 = (f32[4,33,128]{2,1,0:T(8,128)S(1)}, f32[4,33,128]{2,1,0:T(8,128)S(1)}, f32[4,33,128]{2,1,0:T(8,128)S(1)}, f32[4,33,128]{2,1,0:T(8,128)...) fusion(f32[4,33,128]{2,1,0:T(8,128)S(1)} %get-tuple-element.121, ...), kind=kLoop, calls=%fused_computation.207 | loop fusion | flops 19329024 | bytes 5947392 | tf_op jit(solution)/shard_map/add | solution.py:45
  72.3 0.1 fusion.35
  72.5 0.1 fusion.90
  72.6 0.0 collective-permute-done.1
  72.6 0.0 collective-permute-done
  72.6 0.1 pad_maximum_fusion
  72.6 0.1 fusion.27
  72.8 0.2 multiply_add_fusion
  72.9 0.1 maximum_maximum_fusion
  73.1 0.1 fusion.34
  73.2 4.4 %multiply_add_fusion.22 = (f32[5,32,128]{2,1,0:T(8,128)S(1)}, f32[5,32,128]{2,1,0:T(8,128)S(1)}, f32[5,32,128]{2,1,0:T(8,128)S(1)}, f32[5,32,128]{2,1,0:T(8,128)...) fusion(f32[5,32,128]{2,1,0:T(8,128)S(1)} %get-tuple-element.115, f32[5,32,128]{2,1,0:T(8,128)S(1)} %get-tuple-element.114, ...), kind=kLoop, calls=%fused_computation.253 | loop fusion | flops 22937600 | bytes 6553600 | tf_op jit(solution)/shard_map/add | solution.py:45
  77.6 0.1 fusion.37
  77.8 0.9 %multiply_subtract_fusion = f32[5,4,32,128]{3,2,1,0:T(8,128)} fusion(f32[5,4,32,128]{3,2,1,0:T(8,128)S(1)} %get-tuple-element.122, f32[5,4,32,128]{3,2,1,0:T(8,128)S(1)} %fusion.110, f32[5,4,32,128]{3,2,1,0:T(8,128)S(1)} %get-tuple-element.123, f32[]{:T(128)S(6)} %div.735, f32[1,4,32,128]{3,2,1,0:T(8,128)S(1)} %get-tuple-element.117, ...), kind=kLoop, calls=%fused_computation.6 | loop fusion | flops 491520 | bytes 1638404 | tf_op jit(solution)/shard_map/sub | solution.py:202
  (14 shorter events, 0.2 us)
Async XLA Ops:
  0.0 1.0 %copy-start = (f32[4,32,128]{2,1,0:T(8,128)S(1)}, f32[4,32,128]{2,1,0:T(8,128)}, u32[]{:S(2)}) copy-start(f32[4,32,128]{2,1,0:T(8,128)} %param.3) | copy-start | bytes 196612
  0.0 1.0 %copy-start.1 = (f32[4,32,128]{2,1,0:T(8,128)S(1)}, f32[4,32,128]{2,1,0:T(8,128)}, u32[]{:S(2)}) copy-start(f32[4,32,128]{2,1,0:T(8,128)} %param.5) | copy-start | bytes 196612
  1.9 51.9 %collective-permute-start.5 = (f32[5,4,32,3]{3,2,1,0:T(8,128)S(1)}, f32[5,4,32,3]{3,2,1,0:T(8,128)S(1)}, u32[]{:S(2)}, u32[]{:S(2)}) collective-permute-start(f32[5,4,32,3]{3,2,1,0:T(8,128)S(1)} %get-tuple-element.103), channel_id=1, source_target_pairs={{1,0},{0,1},{3,2},{2,3},{5,4},{4,5},{7,6},{6,7},{9,8},{8,9},{11,10... | collective-permute-start | bytes 23048 | tf_op jit(solution)/shard_map/ppermute | solution.py:20
  4.0 53.0 %collective-permute-start.4 = (f32[5,4,32,3]{3,2,1,0:T(8,128)S(1)}, f32[5,4,32,3]{3,2,1,0:T(8,128)S(1)}, u32[]{:S(2)}, u32[]{:S(2)}) collective-permute-start(f32[5,4,32,3]{3,2,1,0:T(8,128)S(1)} %get-tuple-element.102), channel_id=1, source_target_pairs={{0,1},{1,0},{2,3},{3,2},{4,5},{5,4},{6,7},{7,6},{8,9},{9,8},{10,11... | collective-permute-start | bytes 23048 | tf_op jit(solution)/shard_map/ppermute | solution.py:18
  4.1 63.3 %collective-permute-start.3 = (f32[5,4,3,128]{3,2,1,0:T(4,128)S(1)}, f32[5,4,3,128]{3,2,1,0:T(4,128)S(1)}, u32[]{:S(2)}, u32[]{:S(2)}) collective-permute-start(f32[5,4,3,128]{3,2,1,0:T(4,128)S(1)} %get-tuple-element.97), channel_id=1, source_target_pairs={{2,0},{4,2},{6,4},{0,6},{3,1},{5,3},{7,5},{1,7},{10,8},{12,10},{14... | collective-permute-start | bytes 92168 | tf_op jit(solution)/shard_map/ppermute | solution.py:20
  7.6 59.8 %collective-permute-start.2 = (f32[5,4,3,128]{3,2,1,0:T(4,128)S(1)}, f32[5,4,3,128]{3,2,1,0:T(4,128)S(1)}, u32[]{:S(2)}, u32[]{:S(2)}) collective-permute-start(f32[5,4,3,128]{3,2,1,0:T(4,128)S(1)} %get-tuple-element.96), channel_id=1, source_target_pairs={{0,2},{2,4},{4,6},{6,0},{1,3},{3,5},{5,7},{7,1},{8,10},{10,12},{12... | collective-permute-start | bytes 92168 | tf_op jit(solution)/shard_map/ppermute | solution.py:18
  7.7 64.9 %collective-permute-start.1 = (f32[5,3,32,128]{3,2,1,0:T(8,128)S(1)}, f32[5,3,32,128]{3,2,1,0:T(8,128)S(1)}, u32[]{:S(2)}, u32[]{:S(2)}) collective-permute-start(f32[5,3,32,128]{3,2,1,0:T(8,128)S(1)} %get-tuple-element.101), channel_id=1, source_target_pairs={{8,0},{16,8},{24,16},{0,24},{9,1},{17,9},{25,17},{1,25},{10,2},{18... | collective-permute-start | bytes 737288 | tf_op jit(solution)/shard_map/ppermute | solution.py:20
  53.8 18.8 %collective-permute-start = (f32[5,3,32,128]{3,2,1,0:T(8,128)S(1)}, f32[5,3,32,128]{3,2,1,0:T(8,128)S(1)}, u32[]{:S(2)}, u32[]{:S(2)}) collective-permute-start(f32[5,3,32,128]{3,2,1,0:T(8,128)S(1)} %get-tuple-element.100), channel_id=1, source_target_pairs={{0,8},{8,16},{16,24},{24,0},{1,9},{9,17},{17,25},{25,1},{2,10},{10... | collective-permute-start | bytes 737288 | tf_op jit(solution)/shard_map/ppermute | solution.py:18
where the time goes:
time: 79 us; the launch traced here: 78.7 us
  blocking collectives  43.8 us (55%)
  other arithmetic  22.9 us (29%)
  starting transfers between devices  10.5 us (13%)
  between operations  1.02 us (1%)
    pmax x1, blocking collectives, local(): top = lax.pmax(local_top, ('gx', 'gy', 'gz'))  43.8 us
    add x6, other arithmetic, combine(): total = term if total is None else total + term  18.3 us
    ppermute x3, starting transfers between devices, padded_2(): lax.ppermute(head, axis, [((i + 1) % count, i) for i in range(count)])  7.21 us
    ppermute x3, starting transfers between devices, padded_2(): lax.ppermute(tail, axis, [(i, (i + 1) % count) for i in range(count)])  3.31 us
  transfers between devices with their start and end apart: 6, of which 0 were waited for; matrix products, arithmetic and copies ran while one was open for 20% of the time, Pallas kernels for 0%

commit v1 on v0

v1 whole, which is shorter than its diff:
```python
import functools

import jax
import jax.numpy as jnp
from jax import lax
from jax.experimental import pallas as pl
from jax.experimental.pallas import tpu as pltpu
from jax.sharding import PartitionSpec as P

MESH = pl.DeviceIdType.MESH
AXES = ("gx", "gy", "gz")
gamma_gas = 1.4
weno_eps = 1e-06
cfl_number = 0.4
scale = 0.125
eps_outer = 0.75 * 16.0 * scale * scale * weno_eps
eps_inner = 0.75 * 4.0 * scale * scale * weno_eps
ROWS = 8


def rcp(x):
    guess = pl.reciprocal(x, approx=True)
    return guess * (2.0 - x * guess)


def cell_arrays(rho, vn, va, vb, p):
    inv_root = lax.rsqrt(rho)
    root = rho * inv_root
    c2 = gamma_gas * p * (inv_root * inv_root)
    mn, ma, mb = rho * vn, rho * va, rho * vb
    energy = 2.5 * p + 0.5 * (mn * vn + ma * va + mb * vb)
    signal = jnp.abs(vn) + c2 * lax.rsqrt(c2)
    return [
        rho, mn, ma, mb, energy,
        mn * vn + p, ma * vn, mb * vn, (energy + p) * vn,
        root, vn, va, vb, c2, signal,
    ]


def put_cells(ref, row, arrays):
    for k, array in enumerate(arrays):
        ref[k, pl.ds(row, ROWS), :] = array


def weno(d1, d2, d3, d4, eps):
    h2 = (d2 + d2) - d1
    h3 = (d3 + d3) - d4
    e1, e2, e3 = d2 - d1, d3 - d2, d4 - d3
    s2, s3 = 0.75 * d2, 0.75 * d3
    a = (e1 * e1 + s2 * h2) + eps
    b = (e2 * e2 + s2 * d3) + eps
    c = (e3 * e3 + s3 * h3) + eps
    bc, ac, ab = b * c, a * c, a * b
    w0 = bc * bc
    w1 = 6.0 * (ac * ac)
    w2 = 1.5 * (ab * ab)
    den = w0 + w1 + (w2 + w2)
    return (w0 * (h2 - d3) + w2 * (h3 - d2)) * rcp(den)


def face_tile(cells, flux, base, stride, row):
    def load(k, j):
        return cells[k, pl.ds(base + j * stride, ROWS), :]

    sl, sr = load(9, 2), load(9, 3)
    inv = rcp(sl + sr)
    wl, wr = sl * inv, sr * inv
    vl = [load(10 + k, 2) for k in range(3)]
    dv = [load(10 + k, 3) - vl[k] for k in range(3)]
    un, ta, tb = [vl[k] + wr * dv[k] for k in range(3)]
    jump = dv[0] * dv[0] + dv[1] * dv[1] + dv[2] * dv[2]
    c2 = wl * load(13, 2) + wr * load(13, 3) + (0.2 * (wl * wr)) * jump
    ic = lax.rsqrt(c2)
    sound = c2 * ic
    b1 = 0.4 * (ic * ic)
    qh = 0.5 * (un * un + ta * ta + tb * tb)
    enth = 2.5 * c2 + qh
    alpha = load(14, 0)
    for j in range(1, 6):
        alpha = jnp.maximum(alpha, load(14, j))

    state = [[load(k, j) for j in range(6)] for k in range(5)]
    phys = [state[1]] + [[load(k, j) for j in range(6)] for k in range(5, 9)]
    du = [[s[j + 1] - s[j] for j in range(5)] for s in state]
    df = [du[1]] + [[s[j + 1] - s[j] for j in range(5)] for s in phys[1:]]
    au = [[alpha * d for d in s] for s in du]

    def project(r, mn, ma, mb, e):
        s = (un * r - mn) * ic
        z = b1 * (e - un * mn - ta * ma - tb * mb + qh * r)
        return z + s, r - z, ma - ta * r, mb - tb * r, z - s

    plus = [project(*[df[k][j] + au[k][j] for k in range(5)]) for j in range(4)]
    minus = [project(*[df[k][j] - au[k][j] for k in range(5)]) for j in range(1, 5)]
    hats = []
    for k in range(5):
        eps = eps_outer if k in (0, 4) else eps_inner
        up = weno(plus[0][k], plus[1][k], plus[2][k], plus[3][k], eps)
        down = weno(minus[3][k], minus[2][k], minus[1][k], minus[0][k], eps)
        hats.append(up - down)
    lin = []
    for k in range(5):
        centre = 6.0 * (phys[k][2] + phys[k][3]) + (df[k][1] - df[k][3])
        lin.append(centre + ((au[k][1] + au[k][3]) - (au[k][2] + au[k][2])))
    h1, h2, h3, h4, h5 = hats
    h2, h3, h4 = h2 + h2, h3 + h3, h4 + h4
    h15 = h1 + h5
    k5 = sound * (h5 - h1)
    s = h15 + h2
    result = [
        lin[0] + s,
        lin[1] + (un * s + k5),
        lin[2] + (ta * s + h3),
        lin[3] + (tb * s + h4),
        lin[4] + (enth * h15 + un * k5 + qh * h2 + ta * h3 + tb * h4),
    ]
    for k in range(5):
        flux[k, pl.ds(row, ROWS), :] = result[k]


def kernel(
    counts, den, vel, pre, out,
    cx, cy, cz, gx, gy, gz, acc, tz, hx, hy, hz, top, got,
    send_sem, recv_sem, top_send, top_recv,
):
    nx, ny, lanes = den.shape
    nrow = nx * ny
    nz = lanes
    tiles = ny // ROWS
    ypad = ny + 3 * ROWS
    yface = ny + ROWS

    me = [lax.axis_index(a) for a in AXES]
    barrier = pltpu.get_barrier_semaphore()
    peers = []
    for axis, name in enumerate(AXES):
        for k in range(1, counts[axis]):
            peers.append((axis, {name: lax.rem(me[axis] + k, counts[axis])}))
    for _, peer in peers:
        pl.semaphore_signal(barrier, inc=1, device_id=peer, device_id_type=MESH)

    def speed(q, best):
        i, r = q // tiles, pl.multiple_of(lax.rem(q, tiles) * ROWS, ROWS)
        inv_root = lax.rsqrt(den[i, pl.ds(r, ROWS), :])
        c2 = gamma_gas * pre[i, pl.ds(r, ROWS), :] * (inv_root * inv_root)
        total = jnp.abs(vel[0, i, pl.ds(r, ROWS), :]) + jnp.abs(vel[1, i, pl.ds(r, ROWS), :])
        total = total + jnp.abs(vel[2, i, pl.ds(r, ROWS), :])
        return jnp.maximum(best, total + 3.0 * (c2 * lax.rsqrt(c2)))

    top[0] = lax.fori_loop(0, nx * tiles, speed, jnp.zeros((ROWS, lanes), jnp.float32))

    tz[0] = den[...].reshape(nrow, nz).T
    for k in range(3):
        tz[1 + k] = vel[k].reshape(nrow, nz).T
    tz[4] = pre[...].reshape(nrow, nz).T

    pl.semaphore_wait(barrier, len(peers))

    def remote(src, dst, slot, peer):
        copy = pltpu.make_async_remote_copy(
            src_ref=src, dst_ref=dst, send_sem=send_sem.at[slot], recv_sem=recv_sem.at[slot],
            device_id=peer, device_id_type=MESH,
        )
        copy.start()
        return copy

    def send_top(axis):
        copies = []
        for slot, (other, peer) in enumerate(peers):
            if other == axis:
                copy = pltpu.make_async_remote_copy(
                    src_ref=top.at[axis], dst_ref=got.at[slot],
                    send_sem=top_send.at[slot], recv_sem=top_recv.at[slot],
                    device_id=peer, device_id_type=MESH,
                )
                copy.start()
                copies.append((slot, copy))
        return copies

    def take_top(axis, copies):
        best = top[axis]
        for slot, copy in copies:
            copy.wait()
            best = jnp.maximum(best, got[slot])
        top[axis + 1] = best

    def near(axis, way):
        return {AXES[axis]: lax.rem(me[axis] + way + counts[axis], counts[axis])}

    top_x = send_top(0)
    zc = [
        remote(tz.at[:, pl.ds(nz - ROWS, ROWS), :], hz.at[0], 0, near(2, 1)),
        remote(tz.at[:, pl.ds(0, ROWS), :], hz.at[1], 1, near(2, -1)),
    ]
    yc, xc = [], []
    for side, start, way in ((0, ny - ROWS, 1), (1, 0, -1)):
        peer = near(1, way)
        slot = 2 + 3 * side
        yc.append(remote(den.at[:, pl.ds(start, ROWS), :], hy.at[side, 0], slot, peer))
        yc.append(remote(vel.at[:, :, pl.ds(start, ROWS), :], hy.at[side, pl.ds(1, 3)], slot + 1, peer))
        yc.append(remote(pre.at[:, pl.ds(start, ROWS), :], hy.at[side, 4], slot + 2, peer))
    for side, start, way in ((0, nx - 3, 1), (1, 0, -1)):
        peer = near(0, way)
        slot = 8 + 3 * side
        xc.append(remote(den.at[pl.ds(start, 3)], hx.at[side, 0], slot, peer))
        xc.append(remote(vel.at[:, pl.ds(start, 3)], hx.at[side, pl.ds(1, 3)], slot + 1, peer))
        xc.append(remote(pre.at[pl.ds(start, 3)], hx.at[side, 4], slot + 2, peer))

    @pl.loop(0, nz // ROWS)
    def _(t):
        r = pl.multiple_of(t * ROWS, ROWS)
        rho, v1, v2, v3, p = [tz[k, pl.ds(r, ROWS), :] for k in range(5)]
        put_cells(cz, r + ROWS, cell_arrays(scale * rho, v3, v1, v2, scale * p))

    @pl.loop(0, nx * tiles)
    def _(q):
        i, r = q // tiles, pl.multiple_of(lax.rem(q, tiles) * ROWS, ROWS)
        rho = scale * den[i, pl.ds(r, ROWS), :]
        p = scale * pre[i, pl.ds(r, ROWS), :]
        v1, v2, v3 = [vel[k, i, pl.ds(r, ROWS), :] for k in range(3)]
        put_cells(cx, pl.multiple_of(3 * ny + q * ROWS, ROWS), cell_arrays(rho, v1, v2, v3, p))
        put_cells(cy, pl.multiple_of(i * ypad + ROWS + r, ROWS), cell_arrays(rho, v2, v1, v3, p))

    take_top(0, top_x)

    def z_face(t):
        r = pl.multiple_of(t * ROWS, ROWS)
        face_tile(cz, gz, r + 5, 1, r)

    pl.loop(1, nz // ROWS - 1)(z_face)
    top_y = send_top(1)
    for side, row in ((0, 0), (1, nz + ROWS)):
        zc[side].wait()
        rho, v1, v2, v3, p = [hz[side, k] for k in range(5)]
        put_cells(cz, row, cell_arrays(scale * rho, v3, v1, v2, scale * p))

    @pl.loop(0, 3)
    def _(t):
        z_face(jnp.where(t == 0, 0, nz // ROWS - 2 + t))

    for k, field in enumerate((0, 3, 1, 2, 4)):
        acc[field] = (gz[k, pl.ds(1, nz), :] - gz[k, pl.ds(0, nz), :]).T

    take_top(1, top_y)

    for copy in yc:
        copy.wait()
    for side in range(2):
        @pl.loop(0, nx)
        def _(i):
            rho, v1, v2, v3, p = [hy[side, k, i] for k in range(5)]
            row = pl.multiple_of(i * ypad + side * (ny + ROWS), ROWS)
            put_cells(cy, row, cell_arrays(scale * rho, v2, v1, v3, scale * p))

    @pl.loop(0, nx * (tiles + 1))
    def _(q):
        i, t = q // (tiles + 1), lax.rem(q, tiles + 1)
        face_tile(cy, gy, i * ypad + t * ROWS + 5, 1, pl.multiple_of(i * yface + t * ROWS, ROWS))

    top_z = send_top(2)

    for copy in xc:
        copy.wait()
    for side in range(2):
        @pl.loop(0, 3 * tiles)
        def _(q):
            i, r = q // tiles, pl.multiple_of(lax.rem(q, tiles) * ROWS, ROWS)
            rho, v1, v2, v3, p = [hx[side, k, i, pl.ds(r, ROWS), :] for k in range(5)]
            row = pl.multiple_of(side * (nx + 3) * ny + q * ROWS, ROWS)
            put_cells(cx, row, cell_arrays(scale * rho, v1, v2, v3, scale * p))

    @pl.loop(0, (nx + 1) * tiles)
    def _(q):
        r = pl.multiple_of(q * ROWS, ROWS)
        face_tile(cx, gx, r, ny, r)

    take_top(2, top_z)
    largest = jnp.max(top[3], axis=(0, 1), keepdims=True)
    factor = jnp.broadcast_to((cfl_number / (12.0 * scale)) / largest, (ROWS, lanes))

    @pl.loop(0, nx * tiles)
    def _(q):
        i, r = q // tiles, pl.multiple_of(lax.rem(q, tiles) * ROWS, ROWS)
        row = pl.multiple_of(q * ROWS, ROWS)
        yrow = pl.multiple_of(i * yface + r, ROWS)
        for field, k in enumerate((0, 2, 1, 3, 4)):
            total = acc[field, pl.ds(row, ROWS), :]
            total = total + (gy[k, pl.ds(yrow + 1, ROWS), :] - gy[k, pl.ds(yrow, ROWS), :])
            total = total + (gx[field, pl.ds(row + ny, ROWS), :] - gx[field, pl.ds(row, ROWS), :])
            state = cx[field, pl.ds(pl.multiple_of(row + 3 * ny, ROWS), ROWS), :]
            out[field, i, pl.ds(r, ROWS), :] = (1.0 / scale) * state - factor * total


def local(counts, density, velocity, pressure):
    nx, ny, nz = density.shape
    nrow = nx * ny
    npeers = sum(counts) - len(counts)
    f32 = jnp.float32
    vmem = pl.BlockSpec(memory_space=pltpu.VMEM)
    return pl.pallas_call(
        functools.partial(kernel, counts),
        out_shape=jax.ShapeDtypeStruct((5, nx, ny, nz), f32),
        in_specs=[vmem] * 3,
        out_specs=vmem,
        scratch_shapes=[
            pltpu.VMEM((15, (nx + 6) * ny, nz), f32),
            pltpu.VMEM((15, nx * (ny + 3 * ROWS), nz), f32),
            pltpu.VMEM((15, nz + 3 * ROWS, nrow), f32),
            pltpu.VMEM((5, (nx + 1) * ny, nz), f32),
            pltpu.VMEM((5, nx * (ny + ROWS), nz), f32),
            pltpu.VMEM((5, nz + ROWS, nrow), f32),
            pltpu.VMEM((5, nrow, nz), f32),
            pltpu.VMEM((5, nz, nrow), f32),
            pltpu.VMEM((2, 5, 3, ny, nz), f32),
            pltpu.VMEM((2, 5, nx, ROWS, nz), f32),
            pltpu.VMEM((2, 5, ROWS, nrow), f32),
            pltpu.VMEM((4, ROWS, nz), f32),
            pltpu.VMEM((npeers, ROWS, nz), f32),
            pltpu.SemaphoreType.DMA((14,)),
            pltpu.SemaphoreType.DMA((14,)),
            pltpu.SemaphoreType.DMA((npeers,)),
            pltpu.SemaphoreType.DMA((npeers,)),
        ],
        compiler_params=pltpu.CompilerParams(collective_id=0, has_side_effects=True),
    )(density, velocity, pressure)


def solution(mesh):
    counts = tuple(mesh.shape[a] for a in AXES)
    in_specs = (P("gx", "gy", "gz"), P(None, "gx", "gy", "gz"), P("gx", "gy", "gz"))
    out_specs = P(None, "gx", "gy", "gz")
    return jax.shard_map(
        functools.partial(local, counts), mesh=mesh, in_specs=in_specs, out_specs=out_specs, check_vma=False
    )
```

time: 79 us -> 24.2 us (0.31)
  the two profiles are of different devices: /device:TPU:1 before, /device:TPU:0 now
where the time goes in v1:
time: 24.2 us; the launch traced here: 24 us
  Pallas kernels  22.3 us (92%)
  local copies, waits for them, and re-layouts  1.72 us (7%)
    pallas_call x1, Pallas kernels, local(): pl.pallas_call(functools.partial(kernel, counts), out_shape=jax.ShapeDtyp...  22.3 us
    unnamed x1, local copies, waits for them, and re-layouts  1.72 us

profile of v1, /device:TPU:0, one launch (start us, length us, event | category | flops | bytes accessed | tf_op | source)
XLA Modules:
  0.0 24.0 jit_solution(3041733388859978293)
XLA Ops:
  0.0 22.3 %shard_map.37 = f32[5,4,32,128]{3,2,1,0:T(8,128)} custom-call(f32[4,32,128]{2,1,0:T(8,128)} %den.1, f32[3,4,32,128]{3,2,1,0:T(8,128)} %vel.1, f32[4,32,128]{2,1,0:T(8,128)} %pre.1), custom_call_target="tpu_custom_call" | custom-call | tf_op jit(solution)/shard_map/pallas_call | solution.py:300
  22.3 1.7 %copy.5 = f32[5,4,32,128]{3,2,1,0:T(8,128)} copy(f32[5,4,32,128]{3,2,1,0:T(8,128)} %shard_map.37) | data formatting | bytes 655360

commit v2 on v1

--- a/solution.py
+++ b/solution.py
@@ -1,4 +1,6 @@
 import functools
+import itertools
+import math
 
 import jax
 import jax.numpy as jnp
@@ -16,6 +18,7 @@
 eps_outer = 0.75 * 16.0 * scale * scale * weno_eps
 eps_inner = 0.75 * 4.0 * scale * scale * weno_eps
 ROWS = 8
+EARLY = 0
 
 
 def rcp(x):
@@ -23,18 +26,26 @@
     return guess * (2.0 - x * guess)
 
 
-def cell_arrays(rho, vn, va, vb, p):
+def cell_basis(rho, v, p):
     inv_root = lax.rsqrt(rho)
-    root = rho * inv_root
     c2 = gamma_gas * p * (inv_root * inv_root)
-    mn, ma, mb = rho * vn, rho * va, rho * vb
-    energy = 2.5 * p + 0.5 * (mn * vn + ma * va + mb * vb)
-    signal = jnp.abs(vn) + c2 * lax.rsqrt(c2)
+    m = [rho * u for u in v]
+    energy = 2.5 * p + 0.5 * (m[0] * v[0] + m[1] * v[1] + m[2] * v[2])
+    return rho, v, p, m, energy, rho * inv_root, c2, c2 * lax.rsqrt(c2)
+
+
+def cell_arrays(basis, order):
+    rho, v, p, m, energy, root, c2, sound = basis
+    vn, va, vb = [v[k] for k in order]
+    mn, ma, mb = [m[k] for k in order]
     return [
         rho, mn, ma, mb, energy,
         mn * vn + p, ma * vn, mb * vn, (energy + p) * vn,
-        root, vn, va, vb, c2, signal,
+        root, vn, va, vb, c2, jnp.abs(vn) + sound,
     ]
+
+
+FIRST, SECOND, THIRD = (0, 1, 2), (1, 0, 2), (2, 0, 1)
 
 
 def put_cells(ref, row, arrays):
@@ -118,10 +129,16 @@
         flux[k, pl.ds(row, ROWS), :] = result[k]
 
 
+def top_groups(counts):
+    if math.prod(counts) <= 64:
+        return (tuple(range(len(counts))),)
+    return tuple((a,) for a in range(len(counts)))
+
+
 def kernel(
-    counts, den, vel, pre, out,
-    cx, cy, cz, gx, gy, gz, acc, tz, hx, hy, hz, top, got,
-    send_sem, recv_sem, top_send, top_recv,
+    counts, early, den_in, vel_in, pre_in, out,
+    den, vel, pre, cx, cy, cz, gx, gy, gz, acc, tz, hx, hy, hz, top, got,
+    in_sem, send_sem, recv_sem, top_send, top_recv,
 ):
     nx, ny, lanes = den.shape
     nrow = nx * ny
@@ -132,27 +149,70 @@
 
     me = [lax.axis_index(a) for a in AXES]
     barrier = pltpu.get_barrier_semaphore()
+    groups = top_groups(counts)
     peers = []
-    for axis, name in enumerate(AXES):
-        for k in range(1, counts[axis]):
-            peers.append((axis, {name: lax.rem(me[axis] + k, counts[axis])}))
+    for stage, group in enumerate(groups):
+        for shift in itertools.product(*(range(counts[a]) for a in group)):
+            if any(shift):
+                peer = {AXES[a]: lax.rem(me[a] + k, counts[a]) for a, k in zip(group, shift)}
+                peers.append((stage, peer))
     for _, peer in peers:
         pl.semaphore_signal(barrier, inc=1, device_id=peer, device_id_type=MESH)
 
-    def speed(q, best):
-        i, r = q // tiles, pl.multiple_of(lax.rem(q, tiles) * ROWS, ROWS)
-        inv_root = lax.rsqrt(den[i, pl.ds(r, ROWS), :])
-        c2 = gamma_gas * pre[i, pl.ds(r, ROWS), :] * (inv_root * inv_root)
-        total = jnp.abs(vel[0, i, pl.ds(r, ROWS), :]) + jnp.abs(vel[1, i, pl.ds(r, ROWS), :])
-        total = total + jnp.abs(vel[2, i, pl.ds(r, ROWS), :])
-        return jnp.maximum(best, total + 3.0 * (c2 * lax.rsqrt(c2)))
-
-    top[0] = lax.fori_loop(0, nx * tiles, speed, jnp.zeros((ROWS, lanes), jnp.float32))
+    pairs = ((den_in, den), (vel_in, vel), (pre_in, pre))
+    loads = [pltpu.make_async_copy(a, b, in_sem.at[k]) for k, (a, b) in enumerate(pairs)]
+    for copy in loads:
+        copy.start()
+    for copy in loads:
+        copy.wait()
+
+    def speeds(i, best):
+        for t in range(tiles):
+            r = t * ROWS
+            inv_root = lax.rsqrt(den[i, pl.ds(r, ROWS), :])
+            c2 = gamma_gas * pre[i, pl.ds(r, ROWS), :] * (inv_root * inv_root)
+            v1, v2, v3 = [jnp.abs(vel[k, i, pl.ds(r, ROWS), :]) for k in range(3)]
+            best = jnp.maximum(best, ((v1 + v2) + v3) + 3.0 * (c2 * lax.rsqrt(c2)))
+        return best
+
+    best = lax.fori_loop(0, nx, speeds, jnp.zeros((ROWS, lanes), jnp.float32))
+    top[0] = jnp.max(best, axis=0, keepdims=True)
+
+    def own_cells():
+        @pl.loop(0, nx)
+        def _(i):
+            for t in range(tiles):
+                r = t * ROWS
+                rho = scale * den[i, pl.ds(r, ROWS), :]
+                p = scale * pre[i, pl.ds(r, ROWS), :]
+                basis = cell_basis(rho, [vel[k, i, pl.ds(r, ROWS), :] for k in range(3)], p)
+                put_cells(cx, pl.multiple_of((3 + i) * ny + r, ROWS), cell_arrays(basis, FIRST))
+                put_cells(cy, pl.multiple_of(i * ypad + ROWS + r, ROWS), cell_arrays(basis, SECOND))
 
     tz[0] = den[...].reshape(nrow, nz).T
     for k in range(3):
         tz[1 + k] = vel[k].reshape(nrow, nz).T
     tz[4] = pre[...].reshape(nrow, nz).T
+
+    def own_turned():
+        @pl.loop(0, nz // ROWS, unroll=4)
+        def _(t):
+            r = pl.multiple_of(t * ROWS, ROWS)
+            rho, v1, v2, v3, p = [tz[k, pl.ds(r, ROWS), :] for k in range(5)]
+            basis = cell_basis(scale * rho, (v1, v2, v3), scale * p)
+            put_cells(cz, r + ROWS, cell_arrays(basis, THIRD))
+
+    def z_face(t):
+        r = pl.multiple_of(t * ROWS, ROWS)
+        face_tile(cz, gz, r + 5, 1, r)
+
+    def y_face(i, t):
+        face_tile(cy, gy, i * ypad + t * ROWS + 5, 1, pl.multiple_of(i * yface + t * ROWS, ROWS))
+
+    if early >= 1:
+        own_cells()
+    if early >= 2:
+        own_turned()
 
     pl.semaphore_wait(barrier, len(peers))
 
@@ -184,10 +244,16 @@
             best = jnp.maximum(best, got[slot])
         top[axis + 1] = best
 
+    def next_top(stage, copies):
+        if stage >= len(groups) - 1:
+            return copies
+        take_top(stage, copies)
+        return send_top(stage + 1)
+
     def near(axis, way):
         return {AXES[axis]: lax.rem(me[axis] + way + counts[axis], counts[axis])}
 
-    top_x = send_top(0)
+    pending = send_top(0)
     zc = [
         remote(tz.at[:, pl.ds(nz - ROWS, ROWS), :], hz.at[0], 0, near(2, 1)),
         remote(tz.at[:, pl.ds(0, ROWS), :], hz.at[1], 1, near(2, -1)),
@@ -206,33 +272,23 @@
         xc.append(remote(vel.at[:, pl.ds(start, 3)], hx.at[side, pl.ds(1, 3)], slot + 1, peer))
         xc.append(remote(pre.at[pl.ds(start, 3)], hx.at[side, 4], slot + 2, peer))
 
-    @pl.loop(0, nz // ROWS)
-    def _(t):
-        r = pl.multiple_of(t * ROWS, ROWS)
-        rho, v1, v2, v3, p = [tz[k, pl.ds(r, ROWS), :] for k in range(5)]
-        put_cells(cz, r + ROWS, cell_arrays(scale * rho, v3, v1, v2, scale * p))
-
-    @pl.loop(0, nx * tiles)
+    if early < 1:
+        own_cells()
+    if early < 2:
+        own_turned()
+    pl.loop(1, nz // ROWS - 1)(z_face)
+    pending = next_top(0, pending)
+
+    @pl.loop(0, nx * (tiles - 2))
     def _(q):
-        i, r = q // tiles, pl.multiple_of(lax.rem(q, tiles) * ROWS, ROWS)
-        rho = scale * den[i, pl.ds(r, ROWS), :]
-        p = scale * pre[i, pl.ds(r, ROWS), :]
-        v1, v2, v3 = [vel[k, i, pl.ds(r, ROWS), :] for k in range(3)]
-        put_cells(cx, pl.multiple_of(3 * ny + q * ROWS, ROWS), cell_arrays(rho, v1, v2, v3, p))
-        put_cells(cy, pl.multiple_of(i * ypad + ROWS + r, ROWS), cell_arrays(rho, v2, v1, v3, p))
-
-    take_top(0, top_x)
-
-    def z_face(t):
-        r = pl.multiple_of(t * ROWS, ROWS)
-        face_tile(cz, gz, r + 5, 1, r)
-
-    pl.loop(1, nz // ROWS - 1)(z_face)
-    top_y = send_top(1)
+        y_face(q // (tiles - 2), lax.rem(q, tiles - 2) + 1)
+
+    pending = next_top(1, pending)
+
     for side, row in ((0, 0), (1, nz + ROWS)):
         zc[side].wait()
         rho, v1, v2, v3, p = [hz[side, k] for k in range(5)]
-        put_cells(cz, row, cell_arrays(scale * rho, v3, v1, v2, scale * p))
+        put_cells(cz, row, cell_arrays(cell_basis(scale * rho, (v1, v2, v3), scale * p), THIRD))
 
     @pl.loop(0, 3)
     def _(t):
@@ -241,70 +297,72 @@
     for k, field in enumerate((0, 3, 1, 2, 4)):
         acc[field] = (gz[k, pl.ds(1, nz), :] - gz[k, pl.ds(0, nz), :]).T
 
-    take_top(1, top_y)
-
     for copy in yc:
         copy.wait()
     for side in range(2):
-        @pl.loop(0, nx)
-        def _(i):
+        for i in range(nx):
             rho, v1, v2, v3, p = [hy[side, k, i] for k in range(5)]
-            row = pl.multiple_of(i * ypad + side * (ny + ROWS), ROWS)
-            put_cells(cy, row, cell_arrays(scale * rho, v2, v1, v3, scale * p))
-
-    @pl.loop(0, nx * (tiles + 1))
+            row = i * ypad + side * (ny + ROWS)
+            put_cells(cy, row, cell_arrays(cell_basis(scale * rho, (v1, v2, v3), scale * p), SECOND))
+
+    @pl.loop(0, nx * 3)
     def _(q):
-        i, t = q // (tiles + 1), lax.rem(q, tiles + 1)
-        face_tile(cy, gy, i * ypad + t * ROWS + 5, 1, pl.multiple_of(i * yface + t * ROWS, ROWS))
-
-    top_z = send_top(2)
+        t = lax.rem(q, 3)
+        y_face(q // 3, jnp.where(t == 0, 0, tiles - 2 + t))
+
+    pending = next_top(2, pending)
 
     for copy in xc:
         copy.wait()
     for side in range(2):
-        @pl.loop(0, 3 * tiles)
-        def _(q):
-            i, r = q // tiles, pl.multiple_of(lax.rem(q, tiles) * ROWS, ROWS)
-            rho, v1, v2, v3, p = [hx[side, k, i, pl.ds(r, ROWS), :] for k in range(5)]
-            row = pl.multiple_of(side * (nx + 3) * ny + q * ROWS, ROWS)
-            put_cells(cx, row, cell_arrays(scale * rho, v1, v2, v3, scale * p))
+        @pl.loop(0, 3)
+        def _(i):
+            for t in range(tiles):
+                r = t * ROWS
+                rho, v1, v2, v3, p = [hx[side, k, i, pl.ds(r, ROWS), :] for k in range(5)]
+                row = pl.multiple_of((side * (nx + 3) + i) * ny + r, ROWS)
+                put_cells(cx, row, cell_arrays(cell_basis(scale * rho, (v1, v2, v3), scale * p), FIRST))
 
     @pl.loop(0, (nx + 1) * tiles)
     def _(q):
         r = pl.multiple_of(q * ROWS, ROWS)
         face_tile(cx, gx, r, ny, r)
 
-    take_top(2, top_z)
-    largest = jnp.max(top[3], axis=(0, 1), keepdims=True)
+    take_top(len(groups) - 1, pending)
+    largest = jnp.max(top[len(groups)], axis=(0, 1), keepdims=True)
     factor = jnp.broadcast_to((cfl_number / (12.0 * scale)) / largest, (ROWS, lanes))
 
-    @pl.loop(0, nx * tiles)
-    def _(q):
-        i, r = q // tiles, pl.multiple_of(lax.rem(q, tiles) * ROWS, ROWS)
-        row = pl.multiple_of(q * ROWS, ROWS)
-        yrow = pl.multiple_of(i * yface + r, ROWS)
-        for field, k in enumerate((0, 2, 1, 3, 4)):
-            total = acc[field, pl.ds(row, ROWS), :]
-            total = total + (gy[k, pl.ds(yrow + 1, ROWS), :] - gy[k, pl.ds(yrow, ROWS), :])
-            total = total + (gx[field, pl.ds(row + ny, ROWS), :] - gx[field, pl.ds(row, ROWS), :])
-            state = cx[field, pl.ds(pl.multiple_of(row + 3 * ny, ROWS), ROWS), :]
-            out[field, i, pl.ds(r, ROWS), :] = (1.0 / scale) * state - factor * total
+    @pl.loop(0, nx)
+    def _(i):
+        for t in range(tiles):
+            r = t * ROWS
+            row = pl.multiple_of(i * ny + r, ROWS)
+            yrow = pl.multiple_of(i * yface + r, ROWS)
+            for field, k in enumerate((0, 2, 1, 3, 4)):
+                total = acc[field, pl.ds(row, ROWS), :]
+                total = total + (gy[k, pl.ds(yrow + 1, ROWS), :] - gy[k, pl.ds(yrow, ROWS), :])
+                total = total + (gx[field, pl.ds(row + ny, ROWS), :] - gx[field, pl.ds(row, ROWS), :])
+                state = cx[field, pl.ds(pl.multiple_of(row + 3 * ny, ROWS), ROWS), :]
+                out[field, i, pl.ds(r, ROWS), :] = (1.0 / scale) * state - factor * total
 
 
 def local(counts, density, velocity, pressure):
     nx, ny, nz = density.shape
     nrow = nx * ny
-    npeers = sum(counts) - len(counts)
+    npeers = sum(math.prod(counts[a] for a in group) - 1 for group in top_groups(counts))
     f32 = jnp.float32
     vmem = pl.BlockSpec(memory_space=pltpu.VMEM)
     return pl.pallas_call(
-        functools.partial(kernel, counts),
-        out_shape=jax.ShapeDtypeStruct((5, nx, ny, nz), f32),
-        in_specs=[vmem] * 3,
+        functools.partial(kernel, counts, EARLY),
+        out_shape=pltpu.VMEM((5, nx, ny, nz), f32),
+        in_specs=[pl.BlockSpec(memory_space=pl.ANY)] * 3,
         out_specs=vmem,
         scratch_shapes=[
-            pltpu.VMEM((15, (nx + 6) * ny, nz), f32),
-            pltpu.VMEM((15, nx * (ny + 3 * ROWS), nz), f32),
+            pltpu.VMEM((nx, ny, nz), f32),
+            pltpu.VMEM((3, nx, ny, nz), f32),
+            pltpu.VMEM((nx, ny, nz), f32),
+            pltpu.VMEM((15, (nx + 6) * ny + ROWS, nz), f32),
+            pltpu.VMEM((15, nx * (ny + 3 * ROWS) + ROWS, nz), f32),
             pltpu.VMEM((15, nz + 3 * ROWS, nrow), f32),
             pltpu.VMEM((5, (nx + 1) * ny, nz), f32),
             pltpu.VMEM((5, nx * (ny + ROWS), nz), f32),
@@ -314,8 +372,9 @@
             pltpu.VMEM((2, 5, 3, ny, nz), f32),
             pltpu.VMEM((2, 5, nx, ROWS, nz), f32),
             pltpu.VMEM((2, 5, ROWS, nrow), f32),
-            pltpu.VMEM((4, ROWS, nz), f32),
-            pltpu.VMEM((npeers, ROWS, nz), f32),
+            pltpu.VMEM((4, 1, nz), f32),
+            pltpu.VMEM((npeers, 1, nz), f32),
+            pltpu.SemaphoreType.DMA((3,)),
             pltpu.SemaphoreType.DMA((14,)),
             pltpu.SemaphoreType.DMA((14,)),
             pltpu.SemaphoreType.DMA((npeers,)),

time: 24.2 us -> 18.8 us (0.78)
  Pallas kernels: 22.3 us -> 18 us
  local copies, waits for them, and re-layouts: 1.72 us -> 0.73 us
    pallas_call x1, Pallas kernels: 22.3 us -> 18 us  [local(): pl.pallas_call(functools.partial(kernel, counts, EARLY), out_shape=pltpu....]
    unnamed x1, local copies, waits for them, and re-layouts: 1.72 us -> 0.73 us
where the time goes in v2:
time: 18.8 us; the launch traced here: 18.7 us
  Pallas kernels  18 us (96%)
  local copies, waits for them, and re-layouts  0.73 us (4%)
    pallas_call x1, Pallas kernels, local(): pl.pallas_call(functools.partial(kernel, counts, EARLY), out_shape=pltpu....  18 us
    unnamed x1, local copies, waits for them, and re-layouts  0.73 us

profile of v2, /device:TPU:0, one launch (start us, length us, event | category | flops | bytes accessed | tf_op | source)
XLA Modules:
  0.0 18.7 jit_solution(14322582088728547843)
XLA Ops:
  0.0 18.0 %shard_map.37 = f32[5,4,32,128]{3,2,1,0:T(8,128)S(1)} custom-call(f32[4,32,128]{2,1,0:T(8,128)} %den_in.1, f32[3,4,32,128]{3,2,1,0:T(8,128)} %vel_in.1, f32[4,32,128]{2,1,0:T(8,128)} %pre_in.1), custom_call_target="tpu_custom_call" | custom-call | tf_op jit(solution)/shard_map/pallas_call | solution.py:355
  18.0 0.7 %copy.5 = f32[5,4,32,128]{3,2,1,0:T(8,128)} copy(f32[5,4,32,128]{3,2,1,0:T(8,128)S(1)} %shard_map.37) | data formatting | bytes 655360

commit v3 on v2

--- a/solution.py
+++ b/solution.py
@@ -50,7 +50,7 @@
 
 def put_cells(ref, row, arrays):
     for k, array in enumerate(arrays):
-        ref[k, pl.ds(row, ROWS), :] = array
+        ref[k, pl.ds(row, array.shape[0]), :] = array
 
 
 def weno(d1, d2, d3, d4, eps):
@@ -137,7 +137,7 @@
 
 def kernel(
     counts, early, den_in, vel_in, pre_in, out,
-    den, vel, pre, cx, cy, cz, gx, gy, gz, acc, tz, hx, hy, hz, top, got,
+    den, vel, pre, cx, cy, cz, gx, gy, gz, acc, tz, hx, sy, hy, hz, top, got,
     in_sem, send_sem, recv_sem, top_send, top_recv,
 ):
     nx, ny, lanes = den.shape
@@ -188,6 +188,14 @@
                 basis = cell_basis(rho, [vel[k, i, pl.ds(r, ROWS), :] for k in range(3)], p)
                 put_cells(cx, pl.multiple_of((3 + i) * ny + r, ROWS), cell_arrays(basis, FIRST))
                 put_cells(cy, pl.multiple_of(i * ypad + ROWS + r, ROWS), cell_arrays(basis, SECOND))
+
+    for side, start in ((0, ny - 3), (1, 0)):
+        for i in range(nx):
+            rows = [den[i, pl.ds(start, 3), :]]
+            rows += [vel[k, i, pl.ds(start, 3), :] for k in range(3)]
+            rows.append(pre[i, pl.ds(start, 3), :])
+            for k in range(5):
+                sy[side, pl.ds(3 * (k * nx + i), 3), :] = rows[k]
 
     tz[0] = den[...].reshape(nrow, nz).T
     for k in range(3):
@@ -259,15 +267,11 @@
         remote(tz.at[:, pl.ds(0, ROWS), :], hz.at[1], 1, near(2, -1)),
     ]
     yc, xc = [], []
-    for side, start, way in ((0, ny - ROWS, 1), (1, 0, -1)):
-        peer = near(1, way)
-        slot = 2 + 3 * side
-        yc.append(remote(den.at[:, pl.ds(start, ROWS), :], hy.at[side, 0], slot, peer))
-        yc.append(remote(vel.at[:, :, pl.ds(start, ROWS), :], hy.at[side, pl.ds(1, 3)], slot + 1, peer))
-        yc.append(remote(pre.at[:, pl.ds(start, ROWS), :], hy.at[side, 4], slot + 2, peer))
+    for side, way in ((0, 1), (1, -1)):
+        yc.append(remote(sy.at[side], hy.at[side], 2 + side, near(1, way)))
     for side, start, way in ((0, nx - 3, 1), (1, 0, -1)):
         peer = near(0, way)
-        slot = 8 + 3 * side
+        slot = 4 + 3 * side
         xc.append(remote(den.at[pl.ds(start, 3)], hx.at[side, 0], slot, peer))
         xc.append(remote(vel.at[:, pl.ds(start, 3)], hx.at[side, pl.ds(1, 3)], slot + 1, peer))
         xc.append(remote(pre.at[pl.ds(start, 3)], hx.at[side, 4], slot + 2, peer))
@@ -301,8 +305,8 @@
         copy.wait()
     for side in range(2):
         for i in range(nx):
-            rho, v1, v2, v3, p = [hy[side, k, i] for k in range(5)]
-            row = i * ypad + side * (ny + ROWS)
+            rho, v1, v2, v3, p = [hy[side, pl.ds(3 * (k * nx + i), 3), :] for k in range(5)]
+            row = i * ypad + ROWS + (ny if side else -3)
             put_cells(cy, row, cell_arrays(cell_basis(scale * rho, (v1, v2, v3), scale * p), SECOND))
 
     @pl.loop(0, nx * 3)
@@ -370,13 +374,14 @@
             pltpu.VMEM((5, nrow, nz), f32),
             pltpu.VMEM((5, nz, nrow), f32),
             pltpu.VMEM((2, 5, 3, ny, nz), f32),
-            pltpu.VMEM((2, 5, nx, ROWS, nz), f32),
+            pltpu.VMEM((2, pl.cdiv(15 * nx, ROWS) * ROWS, nz), f32),
+            pltpu.VMEM((2, pl.cdiv(15 * nx, ROWS) * ROWS, nz), f32),
             pltpu.VMEM((2, 5, ROWS, nrow), f32),
             pltpu.VMEM((4, 1, nz), f32),
             pltpu.VMEM((npeers, 1, nz), f32),
             pltpu.SemaphoreType.DMA((3,)),
-            pltpu.SemaphoreType.DMA((14,)),
-            pltpu.SemaphoreType.DMA((14,)),
+            pltpu.SemaphoreType.DMA((10,)),
+            pltpu.SemaphoreType.DMA((10,)),
             pltpu.SemaphoreType.DMA((npeers,)),
             pltpu.SemaphoreType.DMA((npeers,)),
         ],

time: 18.8 us -> 18.3 us (0.973)
  Pallas kernels: 18 us -> 17.4 us
    pallas_call x1, Pallas kernels: 18 us -> 17.4 us  [local(): pl.pallas_call(functools.partial(kernel, counts, EARLY), out_shape=pltpu....]
where the time goes in v3:
time: 18.3 us; the launch traced here: 18.1 us
  Pallas kernels  17.4 us (95%)
  local copies, waits for them, and re-layouts  0.73 us (4%)
    pallas_call x1, Pallas kernels, local(): pl.pallas_call(functools.partial(kernel, counts, EARLY), out_shape=pltpu....  17.4 us
    unnamed x1, local copies, waits for them, and re-layouts  0.73 us

profile of v3, /device:TPU:0, one launch (start us, length us, event | category | flops | bytes accessed | tf_op | source)
XLA Modules:
  0.0 18.1 jit_solution(7635730363390120381)
XLA Ops:
  0.0 17.4 %shard_map.37 = f32[5,4,32,128]{3,2,1,0:T(8,128)S(1)} custom-call(f32[4,32,128]{2,1,0:T(8,128)} %den_in.1, f32[3,4,32,128]{3,2,1,0:T(8,128)} %vel_in.1, f32[4,32,128]{2,1,0:T(8,128)} %pre_in.1), custom_call_target="tpu_custom_call" | custom-call | tf_op jit(solution)/shard_map/pallas_call | solution.py:359
  17.4 0.7 %copy.5 = f32[5,4,32,128]{3,2,1,0:T(8,128)} copy(f32[5,4,32,128]{3,2,1,0:T(8,128)S(1)} %shard_map.37) | data formatting | bytes 655360
